TPU v7x, 128 devices: a whole 4x4x4 slice. The times are simulated.
128 devices in a mesh: grp: 4 (over z), kv: 16 (over x, y), tp: 2 (over core).
Axes of the slice: x: 4, y: 4, z: 4, core: 2. Of those that a mesh axis runs over, the one named last changes fastest.
Arguments:
- hidden_states: bfloat16 [512, 4096], P('grp', 'kv'), may hold values from -6 to 6
- attn_gain: float32 [4096], P('kv'), may hold values from 0.25 to 1.75
- mlp_gain: float32 [4096], replicated, may hold values from 0.25 to 1.75
- w_query: bfloat16 [4096, 4096], P('kv', 'tp'), may hold values from -0.09375 to 0.09375
- w_out: bfloat16 [32, 128, 4096], P('tp', 'kv'), may hold values from -1 to 1
- w_gate: bfloat16 [4096, 14336], P(None, ('kv', 'tp')), may hold values from -0.09375 to 0.09375
- w_up: bfloat16 [4096, 14336], P(None, ('kv', 'tp')), may hold values from -0.09375 to 0.09375
- w_down: bfloat16 [14336, 4096], P(('kv', 'tp')), may hold values from -0.046875 to 0.046875
- kv_pool: bfloat16 [1024, 2, 128, 1024], P(('grp', 'kv'), None, None, 'tp'), may hold values from -110 to 110
- resident_cache: bfloat16 [4, 128, 2, 128, 1024], P('grp', 'kv', None, None, 'tp'), may hold values from -110 to 110
- resident_slot: int32 [4, 128], P('grp', 'kv'), may hold values from 0 to 127
- resident_len: int32 [4, 128], P('grp', 'kv'), may hold values from 1 to 128
- new_owner: int32 [4, 256], replicated, may hold values from 0 to 63, as said below
- new_local: int32 [4, 256], replicated, may hold values from 0 to 15
- new_slot: int32 [4, 256], P('grp', 'kv'), may hold values from 0 to 127
- new_len: int32 [4, 256], P('grp', 'kv'), may hold values from 1 to 128
- token_kv: bfloat16 [512, 2, 1024], P('grp', None, 'tp'), may hold values from -6 to 6
Outputs:
- mixed: bfloat16 [512, 4096], P(('grp', 'kv', 'tp'))
- new_cache: bfloat16 [4, 256, 2, 128, 1024], P('grp', 'kv', None, None, 'tp')
Inputs may be any that keep to these rules, and one draw needn't show every extreme that they name: New page c of group g is kept by the device of kv index c // 16 of group g and comes from the device whose index along grp+kv is new_owner[g, c]; every decode device receives exactly 4 new pages from the owners of each grp index; no owner sends more than 1 pages to the devices of one kv index over all groups, so at most 1 to one device; every owner sends each of its 16 pages exactly once.
All inputs are finite; a program needn't handle non-finite values.
Results may differ from a plain program's by a relative error of at most 0.018.
Values may be sent and summed in bfloat16 or wider, within the bound.
A program may use at most 128 MiB of HBM per device.

v0:
```python
import jax
import jax.numpy as jnp
from jax import lax
from jax.sharding import Mesh
from jax.sharding import PartitionSpec as P

D = 4096
HEADS = 32
KV_HEADS = 8
HEAD_DIM = 128
NPR = 4
KV = ("kv_0", "kv_1")
KV_TP = ("kv_0", "kv_1", "tp")
GRP_KV = ("grp", "kv_0", "kv_1")
GRP_KV_TP = ("grp", "kv_0", "kv_1", "tp")
neg_fill = -1e30
norm_eps = 1e-05


def combined_by_axis(shard, axes, combine):
    for axis in axes:
        pieces = jax.tree.map(lambda part: lax.all_gather(part, axis), shard)
        shard = jax.tree.map(lambda part: part[0], pieces)
        for k in range(1, lax.axis_size(axis)):
            shard = combine(shard, jax.tree.map(lambda part: part[k], pieces))
    return shard


def split_up(shard, dim, peers):
    before, after = (shard.shape[:dim], shard.shape[dim + 1 :])
    return jnp.moveaxis(shard.reshape(*before, peers, -1, *after), dim, 0)


def summed_on_arrival(shard, axis, dim):
    tiles = split_up(shard, dim, lax.axis_size(axis))
    arrived = lax.all_to_all(tiles, axis, split_axis=0, concat_axis=0, tiled=True)
    return arrived.astype(jnp.float32).sum(axis=0)


def combine(earlier, later):
    top_a, sum_a, acc_a = earlier
    top_b, sum_b, acc_b = later
    top = jnp.maximum(top_a, top_b)
    fade_a = jnp.exp(top_a - top)
    fade_b = jnp.exp(top_b - top)
    return (
        top,
        sum_a * fade_a + sum_b * fade_b,
        acc_a * fade_a[..., None] + acc_b * fade_b[..., None],
    )


def nth_match(table, wanted, places):
    matched = (table == wanted).astype(jnp.int32)
    ranking = jnp.cumsum(matched, axis=1) - 1
    return (matched[:, None, :] == 1) & (ranking[:, None, :] == places[None, :, None])


def move_pages(kv_pool, new_owner, new_local):
    groups = lax.axis_size("grp")
    ranks = lax.axis_size(KV)
    per_dev = new_owner.shape[1] // ranks
    cap = groups * NPR // ranks
    grp_rank = lax.axis_index("grp")
    kv_rank = lax.axis_index(KV)
    owners = new_owner.reshape(groups * ranks, per_dev)
    myself = grp_rank * ranks + kv_rank
    places = jnp.arange(cap, dtype=jnp.int32)
    mine = lax.dynamic_index_in_dim(owners, myself, 0, keepdims=False)
    order = jnp.arange(per_dev, dtype=jnp.int32)
    by_col = (
        new_owner.reshape(groups, ranks, per_dev)
        .transpose(1, 0, 2)
        .reshape(ranks, groups * per_dev)
    )
    local_col = (
        new_local.reshape(groups, ranks, per_dev)
        .transpose(1, 0, 2)
        .reshape(ranks, groups * per_dev)
    )
    select = nth_match(by_col, myself, places)
    picked = jnp.sum(jnp.where(select, local_col[:, None, :], 0), axis=2)
    outgoing = jnp.take(kv_pool, picked.reshape(-1), axis=0)
    received = lax.all_to_all(outgoing, KV, split_axis=0, concat_axis=0, tiled=True)
    row_here = lax.dynamic_index_in_dim(by_col, kv_rank, 0, keepdims=False)
    sources = grp_rank * ranks + jnp.arange(ranks, dtype=jnp.int32)
    hits = nth_match(
        jnp.broadcast_to(row_here[None, :], (ranks, row_here.shape[0])), sources[:, None], places
    )
    spots = jnp.arange(row_here.shape[0], dtype=jnp.int32)
    where_f = jnp.sum(jnp.where(hits, spots[None, None, :], 0), axis=2).reshape(-1)
    dest_grp = where_f // per_dev
    dest_pos = where_f % per_dev
    same = (dest_grp[:, None] == dest_grp[None, :]) & (dest_pos[:, None] < dest_pos[None, :])
    rank_in = jnp.sum(same.astype(jnp.int32), axis=0)
    target = dest_grp * NPR + rank_in
    items = jnp.arange(target.shape[0], dtype=jnp.int32)
    inverse = jnp.sum(jnp.where(target[None, :] == items[:, None], items[None, :], 0), axis=1)
    sorted_pages = jnp.take(received, inverse, axis=0)
    arrived = lax.all_to_all(sorted_pages, "grp", split_axis=0, concat_axis=0, tiled=True)
    src_grp = mine // ranks
    earlier = (src_grp[:, None] == src_grp[None, :]) & (order[:, None] < order[None, :])
    before = jnp.sum(earlier.astype(jnp.int32), axis=0)
    return jnp.take(arrived, src_grp * NPR + before, axis=0)


def local_partials(query, resident, arrived, res_slot, res_len, arr_slot, arr_len, token_kv, first):
    pages = jnp.concatenate([resident, arrived], axis=0)
    owner_slot = jnp.concatenate([res_slot, arr_slot])
    filled = jnp.concatenate([res_len, arr_len])
    count = pages.shape[0]
    tokens = pages.shape[2]
    kv_here = pages.shape[3] // HEAD_DIM
    slots = query.shape[0]
    ratio = HEADS // KV_HEADS
    keys = pages[:, 0].astype(jnp.float32).reshape(count, tokens, kv_here, HEAD_DIM)
    values = pages[:, 1].astype(jnp.float32).reshape(count, tokens, kv_here, HEAD_DIM)
    grouped = query.reshape(slots, kv_here, ratio, HEAD_DIM)
    picked = jnp.take(grouped, owner_slot, axis=0)
    scores = jnp.einsum("ikgd,itkd->ikgt", picked, keys, precision=lax.Precision.HIGHEST)
    usable = (jnp.arange(tokens, dtype=jnp.int32)[None, :] < filled[:, None])[:, None, None, :]
    scores = jnp.where(usable, scores, neg_fill)
    page_top = jnp.max(scores, axis=3)
    member = owner_slot[None, :] == jnp.arange(slots, dtype=jnp.int32)[:, None]
    slot_top = jnp.max(jnp.where(member[:, :, None, None], page_top[None], neg_fill), axis=1)
    own_keys = token_kv[:, 0].astype(jnp.float32).reshape(slots, kv_here, HEAD_DIM)
    own_values = token_kv[:, 1].astype(jnp.float32).reshape(slots, kv_here, HEAD_DIM)
    own_score = jnp.einsum("skgd,skd->skg", grouped, own_keys, precision=lax.Precision.HIGHEST)
    own_score = jnp.where(first, own_score, neg_fill)
    slot_top = jnp.maximum(slot_top, own_score)
    reach = jnp.take(slot_top, owner_slot, axis=0)
    weights = jnp.where(usable, jnp.exp(scores - reach[..., None]), 0.0)
    page_sum = jnp.sum(weights, axis=3)
    page_acc = jnp.einsum("ikgt,itkd->ikgd", weights, values, precision=lax.Precision.HIGHEST)
    own_weight = jnp.where(first, jnp.exp(own_score - slot_top), 0.0)
    member_f = member.astype(jnp.float32)
    total = jnp.dot(member_f, page_sum.reshape(count, -1), precision=lax.Precision.HIGHEST)
    total = total + own_weight.reshape(slots, -1)
    weighted = jnp.dot(member_f, page_acc.reshape(count, -1), precision=lax.Precision.HIGHEST)
    weighted = (
        weighted.reshape(slots, kv_here, ratio, HEAD_DIM)
        + own_weight[..., None] * own_values[:, :, None, :]
    )
    return (slot_top.reshape(slots, -1), total, weighted.reshape(slots, kv_here * ratio, HEAD_DIM))


def per_device(
    hidden_states,
    attn_gain,
    mlp_gain,
    w_query,
    w_out,
    w_gate,
    w_up,
    w_down,
    kv_pool,
    resident_cache,
    resident_slot,
    resident_len,
    new_owner,
    new_local,
    new_slot,
    new_len,
    token_kv,
):
    ranks = lax.axis_size(KV)
    pairs = lax.axis_size("tp")
    kv_rank = lax.axis_index(KV)
    tp_rank = lax.axis_index("tp")
    features = hidden_states.astype(jnp.float32)
    partial_query = jnp.dot(
        (features * attn_gain).astype(jnp.bfloat16), w_query, preferred_element_type=jnp.float32
    )
    squares = jnp.sum(features * features, axis=1)
    partial_query, squares = lax.psum((partial_query, squares), KV)
    attn_scale = lax.rsqrt(squares / D + norm_eps)
    query = partial_query * attn_scale[:, None] * HEAD_DIM ** (-0.5)
    new_pages = move_pages(kv_pool, new_owner, new_local)
    top, total, weighted = local_partials(
        query,
        resident_cache[0],
        new_pages,
        resident_slot[0],
        resident_len[0],
        new_slot[0],
        new_len[0],
        token_kv,
        kv_rank == 0,
    )
    top, total, weighted = combined_by_axis((top, total, weighted), KV, combine)
    attn = (weighted / total[..., None]).astype(jnp.bfloat16)
    slots = attn.shape[0]
    heads_here = attn.shape[1]
    span = HEAD_DIM // ranks
    piece = lax.dynamic_slice_in_dim(attn, kv_rank * span, span, 2)
    branch = jnp.dot(
        piece.reshape(slots, heads_here * span),
        w_out.reshape(heads_here * span, w_out.shape[2]),
        preferred_element_type=jnp.float32,
    )
    width_here = hidden_states.shape[1]
    laid = branch.reshape(slots, ranks, width_here)
    spot = (jnp.arange(ranks, dtype=jnp.int32) == kv_rank) & (tp_rank == 0)
    laid = laid + jnp.where(spot[None, :, None], features[:, None, :], 0.0)
    resid = lax.psum(laid.reshape(slots, ranks * width_here).astype(jnp.bfloat16), KV_TP)
    resid_f = resid.astype(jnp.float32)
    mlp_scale = lax.rsqrt(jnp.sum(resid_f * resid_f, axis=1) / D + norm_eps)
    normed_mlp = (resid_f * mlp_gain).astype(jnp.bfloat16)
    gate = jnp.dot(normed_mlp, w_gate, preferred_element_type=jnp.float32) * mlp_scale[:, None]
    upward = jnp.dot(normed_mlp, w_up, preferred_element_type=jnp.float32) * mlp_scale[:, None]
    hidden_units = (jax.nn.silu(gate) * upward).astype(jnp.bfloat16)
    row_count = slots // (ranks * pairs)
    down = summed_on_arrival(
        jnp.dot(hidden_units, w_down, preferred_element_type=jnp.float32).astype(jnp.bfloat16),
        KV_TP,
        0,
    )
    row_start = (kv_rank * pairs + tp_rank) * row_count
    kept = lax.dynamic_slice_in_dim(resid_f, row_start, row_count, 0)
    mixed = (kept + down).astype(jnp.bfloat16)
    return (mixed, new_pages[None])


def solution(mesh):
    finer = Mesh(
        mesh.devices.reshape(mesh.shape["grp"], 4, 4, mesh.shape["tp"]),
        ("grp", "kv_0", "kv_1", "tp"),
    )
    return jax.shard_map(
        per_device,
        mesh=finer,
        in_specs=(
            P("grp", KV),
            P(KV),
            P(),
            P(KV, "tp"),
            P("tp", KV, None),
            P(None, KV_TP),
            P(None, KV_TP),
            P(KV_TP, None),
            P(GRP_KV, None, None, "tp"),
            P("grp", KV, None, None, "tp"),
            P("grp", KV),
            P("grp", KV),
            P(),
            P(),
            P("grp", KV),
            P("grp", KV),
            P("grp", None, "tp"),
        ),
        out_specs=(P(GRP_KV_TP, None), P("grp", KV, None, None, "tp")),
        check_vma=False,
    )
```

profile of v0, /device:TPU:1, one launch (start us, length us, event | category | flops | bytes accessed | tf_op | source)
XLA Modules:
  0.0 507.7 jit_solution(3619202428460434715)
XLA Ops:
  10.4 5.0 gather_fusion.2
  20.1 7.6 %all-to-all-start = ((bf16[16,2,128,512]{3,2,1,0:T(8,128)(2,1)}), bf16[16,2,128,512]{3,2,1,0:T(8,128)(2,1)}, u32[]{:S(2)}, u32[]{:S(2)}) async-start(bf16[16,2,128,512]{3,2,1,0:T(8,128)(2,1)} %broadcast_select_fusion.2), calls=%async_computation | async-start | bytes 8388608 | tf_op jit(solution)/shard_map/all_to_all | solution.py:84
  28.5 59.5 %all-to-all-done = bf16[16,2,128,512]{3,2,1,0:T(8,128)(2,1)} async-done(((bf16[16,2,128,512]{3,2,1,0:T(8,128)(2,1)}), bf16[16,2,128,512]{3,2,1,0:T(8,128)(2,1)}, u32[]{:S(2)}, u32[]{:S(2)}) %all-to-all-start) | async-done | bytes 4194336 | tf_op jit(solution)/shard_map/all_to_all | solution.py:84
  88.1 5.0 gather_fusion.3
  93.1 4.7 broadcast_select_fusion.1
  97.8 5.2 %all-to-all-start.1 = ((bf16[16,2,128,512]{3,2,1,0:T(8,128)(2,1)}), bf16[16,2,128,512]{3,2,1,0:T(8,128)(2,1)}, u32[]{:S(2)}, u32[]{:S(2)}) async-start(bf16[16,2,128,512]{3,2,1,0:T(8,128)(2,1)} %broadcast_select_fusion.1), calls=%async_computation.1 | async-start | bytes 8388608 | tf_op jit(solution)/shard_map/all_to_all | solution.py:100
  105.6 33.9 %psum.22 = f32[128]{0:T(128)S(1)} all-reduce(f32[128]{0:T(128)S(1)} %multiply_reduce_fusion.1), channel_id=1, replica_groups=mesh['grp'=4,'kv_0'=4,'kv_1'=4,'tp'=2] {'kv_0','kv_1'}, use_global_device_ids=true, to_apply=%region_2.0 | all-reduce | flops 128 | bytes 1024 | tf_op jit(solution)/shard_map/psum | solution.py:175
  139.8 61.1 %all-reduce.3.cloned.1.call-done = f32[128,2048]{1,0:T(8,128)} async-done(((f32[128,2048]{1,0:T(8,128)}), f32[128,2048]{1,0:T(8,128)}) %all-reduce.3.cloned.1.call-update) | async-done | bytes 1048592 | tf_op jit(solution)/shard_map/psum | solution.py:175
  205.5 5.0 gather_fusion.4
  216.3 4.7 copy.150
  227.0 4.7 copy.155
  231.7 6.9 %fusion.17 = f32[24,4,4,128]{3,2,1,0:T(4,128)S(1)} fusion(bf16[24,128,4,128]{1,3,2,0:T(8,128)(2,1)} %bitcast.217, f32[24,4,4,128]{3,2,1,0:T(4,128)S(1)} %get-tuple-element.40, f32[24,4,4]{2,1,0:T(4,128)S(1)} %broadcast_select_fusion.3, pred[24,128]{1,0:T(8,128)(4,1)S(1)} %iota_compare_fusion), kind=kOutput, calls=%fused_computation.52 | convolution fusion | flops 75595776 | bytes 3543552 | tf_op jit(solution)/shard_map/ikgt,itkd->ikgd/dot_general | solution.py:134
  241.4 9.3 %all_gather.25 = f32[4,128,16]{1,2,0:T(8,128)S(1)} all-gather(f32[1,128,16]{1,2,0:T(8,128)S(1)} %bitcast.229), channel_id=1, replica_groups=mesh['grp'=4,'kv_0'=4,'kv_1'=4,'tp'=2] {'kv_0'}, dimensions={0}, use_global_device_ids=true | all-gather | bytes 40960 | tf_op jit(solution)/shard_map/all_gather | solution.py:22
  251.3 38.9 %all-gather.4.cloned.1.call-done = f32[4,128,16,128]{3,2,1,0:T(8,128)} async-done(((f32[1,128,16,128]{3,2,1,0:T(8,128)}), f32[4,128,16,128]{3,2,1,0:T(8,128)}) %all-gather.4.cloned.1.call-update) | async-done | bytes 4194320 | tf_op jit(solution)/shard_map/all_gather | solution.py:22
  290.2 4.8 fusion.3
  297.1 9.0 %all-gather = f32[512,16]{0,1:T(8,128)S(1)} all-gather(f32[128,16]{0,1:T(8,128)S(1)} %convolution_add_fusion.1), channel_id=2, replica_groups=mesh['grp'=4,'kv_0'=4,'kv_1'=4,'tp'=2] {'kv_0'}, dimensions={0}, use_global_device_ids=true | all-gather | bytes 40960 | tf_op jit(solution)/shard_map/all_gather | solution.py:22
  306.2 10.8 %all_gather.27 = f32[4,128,16]{1,2,0:T(8,128)S(1)} all-gather(f32[1,128,16]{1,2,0:T(8,128)S(1)} %get-tuple-element.15), channel_id=1, replica_groups=mesh['grp'=4,'kv_0'=4,'kv_1'=4,'tp'=2] {'kv_1'}, dimensions={0}, use_global_device_ids=true | all-gather | bytes 40960 | tf_op jit(solution)/shard_map/all_gather | solution.py:22
  317.0 10.6 %all_gather.30 = f32[4,128,16]{1,2,0:T(8,128)S(1)} all-gather(f32[1,128,16]{1,2,0:T(8,128)S(1)} %get-tuple-element.14), channel_id=1, replica_groups=mesh['grp'=4,'kv_0'=4,'kv_1'=4,'tp'=2] {'kv_1'}, dimensions={0}, use_global_device_ids=true | all-gather | bytes 40960 | tf_op jit(solution)/shard_map/all_gather | solution.py:22
  327.6 16.7 %all-gather.6.cloned.1.call-done = f32[4,128,16,128]{3,2,1,0:T(8,128)} async-done(((f32[1,128,16,128]{3,2,1,0:T(8,128)}), f32[4,128,16,128]{3,2,1,0:T(8,128)}) %all-gather.6.cloned.1.call-update) | async-done | bytes 4194320 | tf_op jit(solution)/shard_map/all_gather | solution.py:22
  358.2 105.7 %all-reduce.5.cloned.1.call-done = bf16[128,4096]{1,0:T(8,128)(2,1)} async-done(((bf16[128,4096]{1,0:T(8,128)(2,1)}), bf16[128,4096]{1,0:T(8,128)(2,1)}) %all-reduce.5.cloned.1.call-update) | async-done | bytes 1048592 | tf_op jit(solution)/shard_map/psum | solution.py:205
  469.0 6.0 %convolution_convert_fusion = bf16[128,4096]{1,0:T(8,128)(2,1)S(1)} fusion(bf16[448,4096]{1,0:T(8,128)(2,1)} %param.26, bf16[4096,448]{0,1:T(8,128)(2,1)} %param.25, f32[4096]{0:T(1024)S(1)} %copy-done.7, bf16[128,4096]{1,0:T(8,128)(2,1)S(1)} %copy-done.2, f32[128,448]{0,1:T(8,128)S(1)} %convolution_multiply_fusion.1, f32[128]{0:T(128)S(1)} %add_rsqrt_fusion), kind=kOutput, calls=%fused_computation.7 | convolution fusion | flops 942022656 | bytes 9683456 | tf_op jit(solution)/shard_map/dot_general | solution.py:214
  476.3 6.1 %all-to-all-start.2 = ((bf16[32,4,4096]{2,1,0:T(4,128)(2,1)}), bf16[32,4,4096]{2,1,0:T(4,128)(2,1)S(1)}, u32[]{:S(2)}, u32[]{:S(2)}) async-start(bf16[32,4,4096]{2,1,0:T(4,128)(2,1)} %reshape.671), calls=%async_computation.2 | async-start | bytes 2097152 | tf_op jit(solution)/shard_map/all_to_all | solution.py:36
  482.3 4.8 fusion.92
  488.7 10.6 %all-to-all-done.2 = bf16[32,4,4096]{2,1,0:T(4,128)(2,1)S(1)} async-done(((bf16[32,4,4096]{2,1,0:T(4,128)(2,1)}), bf16[32,4,4096]{2,1,0:T(4,128)(2,1)S(1)}, u32[]{:S(2)}, u32[]{:S(2)}) %all-to-all-start.2) | async-done | bytes 1048608 | tf_op jit(solution)/shard_map/all_to_all | solution.py:36
  (129 shorter events, 57.0 us)
Async XLA Ops:
  7.2 95.8 %copy-start = (bf16[256,2048]{1,0:T(8,128)(2,1)S(1)}, bf16[256,2048]{1,0:T(8,128)(2,1)}, u32[]{:S(2)}) copy-start(bf16[256,2048]{1,0:T(8,128)(2,1)} %param.22) | copy-start | bytes 3145732
  20.1 68.0 %all-to-all-start = ((bf16[16,2,128,512]{3,2,1,0:T(8,128)(2,1)}), bf16[16,2,128,512]{3,2,1,0:T(8,128)(2,1)}, u32[]{:S(2)}, u32[]{:S(2)}) async-start(bf16[16,2,128,512]{3,2,1,0:T(8,128)(2,1)} %broadcast_select_fusion.2), calls=%async_computation | async-start | bytes 8388608 | tf_op jit(solution)/shard_map/all_to_all | solution.py:84
  97.8 5.3 %copy-start.6 = (bf16[128,256]{1,0:T(8,128)(2,1)S(1)}, bf16[128,256]{1,0:T(8,128)(2,1)}, u32[]{:S(2)}) copy-start(bf16[128,256]{1,0:T(8,128)(2,1)} %param.19) | copy-start | bytes 196612
  97.8 5.3 %copy-start.8 = (f32[256]{0:T(256)S(1)}, f32[256]{0:T(256)}, u32[]{:S(2)}) copy-start(f32[256]{0:T(256)} %param.20) | copy-start | bytes 3076
  97.8 6.7 %copy-start.9 = (s32[1,16]{1,0:T(1,128)S(1)}, s32[1,16]{1,0:T(1,128)}, u32[]{:S(2)}) copy-start(s32[1,16]{1,0:T(1,128)} %param.33) | copy-start | bytes 196
  97.8 6.7 %copy-start.10 = (s32[1,8]{1,0:T(1,128)S(1)}, s32[1,8]{1,0:T(1,128)}, u32[]{:S(2)}) copy-start(s32[1,8]{1,0:T(1,128)} %param.29) | copy-start | bytes 100
  97.8 7.0 %copy-start.5 = (bf16[128,2,512]{2,1,0:T(2,128)(2,1)S(1)}, bf16[128,2,512]{2,1,0:T(2,128)(2,1)}, u32[]{:S(2)}) copy-start(bf16[128,2,512]{2,1,0:T(2,128)(2,1)} %param.35) | copy-start | bytes 786436
  97.8 107.8 %all-to-all-start.1 = ((bf16[16,2,128,512]{3,2,1,0:T(8,128)(2,1)}), bf16[16,2,128,512]{3,2,1,0:T(8,128)(2,1)}, u32[]{:S(2)}, u32[]{:S(2)}) async-start(bf16[16,2,128,512]{3,2,1,0:T(8,128)(2,1)} %broadcast_select_fusion.1), calls=%async_computation.1 | async-start | bytes 8388608 | tf_op jit(solution)/shard_map/all_to_all | solution.py:100
  103.0 2.2 copy-start.11
  103.0 2.2 copy-start.12
  103.0 98.0 %all-reduce.3.cloned.1.call-start = ((), (), s32[]{:S(2)}) async-start(), calls=%async_computation.3 | async-start | bytes 2097152 | tf_op jit(solution)/shard_map/psum | solution.py:175
  104.4 185.8 %all-gather.4.cloned.1.call-start = ((), (), s32[]{:S(2)}) async-start(), calls=%async_computation.4 | async-start | bytes 5242880 | tf_op jit(solution)/shard_map/all_gather | solution.py:22
  210.6 2.9 copy-start.3
  241.2 103.0 %all-gather.6.cloned.1.call-start = ((), (), s32[]{:S(2)}) async-start(), calls=%async_computation.5 | async-start | bytes 5242880 | tf_op jit(solution)/shard_map/all_gather | solution.py:22
  250.7 44.4 %copy-start.4 = (bf16[16,8,4096]{2,1,0:T(8,128)(2,1)S(1)}, bf16[16,8,4096]{2,1,0:T(8,128)(2,1)}, u32[]{:S(2)}) copy-start(bf16[16,8,4096]{2,1,0:T(8,128)(2,1)} %param.23) | copy-start | bytes 3145732
  295.0 168.9 %all-reduce.5.cloned.1.call-start = ((), (), s32[]{:S(2)}) async-start(), calls=%async_computation.6 | async-start | bytes 2097152 | tf_op jit(solution)/shard_map/psum | solution.py:205
  356.2 109.3 %copy-start.7 = (f32[4096]{0:T(1024)S(1)}, f32[4096]{0:T(1024)}, u32[]{:S(2)}) copy-start(f32[4096]{0:T(1024)} %param.21) | copy-start | bytes 49156
  463.9 5.1 %copy-start.2 = (bf16[128,4096]{1,0:T(8,128)(2,1)S(1)}, bf16[128,4096]{1,0:T(8,128)(2,1)}, u32[]{:S(2)}) copy-start(bf16[128,4096]{1,0:T(8,128)(2,1)} %all-reduce.5.cloned.1.call-done) | copy-start | bytes 3145732
  476.3 23.0 %all-to-all-start.2 = ((bf16[32,4,4096]{2,1,0:T(4,128)(2,1)}), bf16[32,4,4096]{2,1,0:T(4,128)(2,1)S(1)}, u32[]{:S(2)}, u32[]{:S(2)}) async-start(bf16[32,4,4096]{2,1,0:T(4,128)(2,1)} %reshape.671), calls=%async_computation.2 | async-start | bytes 2097152 | tf_op jit(solution)/shard_map/all_to_all | solution.py:36
  482.3 18.9 %copy-start.1 = (bf16[256,2048]{1,0:T(8,128)(2,1)S(1)}, bf16[256,2048]{1,0:T(8,128)(2,1)}, u32[]{:S(2)}) copy-start(bf16[256,2048]{1,0:T(8,128)(2,1)} %param.22) | copy-start | bytes 3145732
Sparse Core Ops, SparseCore 0:
  107.0 93.8 all-reduce.2
  241.4 48.7 all-gather.3
  295.1 49.0 all-gather.5
  358.4 105.4 all-reduce.4
where the time goes:
time: 509 us; the launch traced here: 508 us
  waiting for transfers between devices  292 us (57%)
  blocking collectives  73.6 us (14%)
  local copies, waits for them, and re-layouts  47 us (9%)
  other arithmetic  34.5 us (7%)
  matrix products  26.8 us (5%)
  starting transfers between devices  19 us (4%)
  between operations  14.2 us (3%)
    psum x1, waiting for transfers between devices, per_device(): lax.psum(laid.reshape(slots, ranks * width_here).astype(jnp.bfloat16), KV...  106 us
    psum x1, waiting for transfers between devices, per_device(): partial_query, squares = lax.psum((partial_query, squares), KV)  61.1 us
    all_to_all x1, waiting for transfers between devices, move_pages(): lax.all_to_all(outgoing, KV, split_axis=0, concat_axis=0, tiled=True)  59.5 us
    all_gather x2, waiting for transfers between devices, combined_by_axis(): pieces = jax.tree.map(lambda part: lax.all_gather(part, axis), shard)  55.5 us
    all_gather x4, blocking collectives, combined_by_axis(): pieces = jax.tree.map(lambda part: lax.all_gather(part, axis), shard)  39.7 us
    psum x1, blocking collectives, per_device(): partial_query, squares = lax.psum((partial_query, squares), KV)  33.9 us
    all_to_all x1, waiting for transfers between devices, summed_on_arrival(): lax.all_to_all(tiles, axis, split_axis=0, concat_axis=0, tiled=True)  10.6 us
  transfers between devices with their start and end apart: 7, of which 6 were waited for; matrix products, arithmetic and copies ran while one was open for 3% of the time, Pallas kernels for 0%

commit v1 on v0

--- a/solution.py
+++ b/solution.py
@@ -1,3 +1,4 @@
+import functools
 import jax
 import jax.numpy as jnp
 from jax import lax
@@ -15,6 +16,15 @@
 GRP_KV_TP = ("grp", "kv_0", "kv_1", "tp")
 neg_fill = -1e30
 norm_eps = 1e-05
+
+
+def get_scenes_on_mesh(v0, dev_axis, chip_axis):
+    for jj in (dev_axis, chip_axis):
+        v0 = jax.lax.psum(v0, jj)
+    return v0
+
+
+create_islands = functools.partial(get_scenes_on_mesh, dev_axis=("kv_1", "tp"), chip_axis="kv_0")
 
 
 def combined_by_axis(shard, axes, combine):
@@ -202,7 +212,7 @@
     laid = branch.reshape(slots, ranks, width_here)
     spot = (jnp.arange(ranks, dtype=jnp.int32) == kv_rank) & (tp_rank == 0)
     laid = laid + jnp.where(spot[None, :, None], features[:, None, :], 0.0)
-    resid = lax.psum(laid.reshape(slots, ranks * width_here).astype(jnp.bfloat16), KV_TP)
+    resid = create_islands(laid.reshape(slots, ranks * width_here).astype(jnp.bfloat16))
     resid_f = resid.astype(jnp.float32)
     mlp_scale = lax.rsqrt(jnp.sum(resid_f * resid_f, axis=1) / D + norm_eps)
     normed_mlp = (resid_f * mlp_gain).astype(jnp.bfloat16)

time: 509 us -> 515 us (1.012)
    psum x1 -> x2, waiting for transfers between devices: 106 us -> 109 us  [get_scenes_on_mesh(): v0 = jax.lax.psum(v0, jj)]
  transfers between devices with their start and end apart: 7 -> 8, of which waited for: 6 -> 7; matrix products, arithmetic and copies ran while one was open for 3% -> 3% of each run, Pallas kernels for 0% -> 0%
where the time goes in v1:
time: 515 us; the launch traced here: 514 us
  waiting for transfers between devices  296 us (57%)
  blocking collectives  73.6 us (14%)
  local copies, waits for them, and re-layouts  47 us (9%)
  other arithmetic  34.5 us (7%)
  matrix products  26.8 us (5%)
  starting transfers between devices  22 us (4%)
  between operations  14.2 us (3%)
    psum x2, waiting for transfers between devices, get_scenes_on_mesh(): v0 = jax.lax.psum(v0, jj)  109 us
    psum x1, waiting for transfers between devices, per_device(): partial_query, squares = lax.psum((partial_query, squares), KV)  61.1 us
    all_to_all x1, waiting for transfers between devices, move_pages(): lax.all_to_all(outgoing, KV, split_axis=0, concat_axis=0, tiled=True)  59.5 us
    all_gather x2, waiting for transfers between devices, combined_by_axis(): pieces = jax.tree.map(lambda part: lax.all_gather(part, axis), shard)  55.5 us
    all_gather x4, blocking collectives, combined_by_axis(): pieces = jax.tree.map(lambda part: lax.all_gather(part, axis), shard)  39.7 us
    psum x1, blocking collectives, per_device(): partial_query, squares = lax.psum((partial_query, squares), KV)  33.9 us
    all_to_all x1, waiting for transfers between devices, summed_on_arrival(): lax.all_to_all(tiles, axis, split_axis=0, concat_axis=0, tiled=True)  10.6 us
  transfers between devices with their start and end apart: 8, of which 7 were waited for; matrix products, arithmetic and copies ran while one was open for 3% of the time, Pallas kernels for 0%

profile of v1, /device:TPU:1, one launch (start us, length us, event | category | flops | bytes accessed | tf_op | source)
XLA Modules:
  0.0 514.1 jit_solution(12943408778276043741)
XLA Ops:
  10.4 5.0 gather_fusion.2
  20.1 7.6 %all-to-all-start = ((bf16[16,2,128,512]{3,2,1,0:T(8,128)(2,1)}), bf16[16,2,128,512]{3,2,1,0:T(8,128)(2,1)}, u32[]{:S(2)}, u32[]{:S(2)}) async-start(bf16[16,2,128,512]{3,2,1,0:T(8,128)(2,1)} %broadcast_select_fusion.2), calls=%async_computation | async-start | bytes 8388608 | tf_op jit(solution)/shard_map/all_to_all | solution.py:94
  28.5 59.5 %all-to-all-done = bf16[16,2,128,512]{3,2,1,0:T(8,128)(2,1)} async-done(((bf16[16,2,128,512]{3,2,1,0:T(8,128)(2,1)}), bf16[16,2,128,512]{3,2,1,0:T(8,128)(2,1)}, u32[]{:S(2)}, u32[]{:S(2)}) %all-to-all-start) | async-done | bytes 4194336 | tf_op jit(solution)/shard_map/all_to_all | solution.py:94
  88.1 5.0 gather_fusion.3
  97.8 5.2 %all-to-all-start.1 = ((bf16[16,2,128,512]{3,2,1,0:T(8,128)(2,1)}), bf16[16,2,128,512]{3,2,1,0:T(8,128)(2,1)}, u32[]{:S(2)}, u32[]{:S(2)}) async-start(bf16[16,2,128,512]{3,2,1,0:T(8,128)(2,1)} %broadcast_select_fusion.1), calls=%async_computation.1 | async-start | bytes 8388608 | tf_op jit(solution)/shard_map/all_to_all | solution.py:110
  105.6 33.9 %psum.29 = f32[128]{0:T(128)S(1)} all-reduce(f32[128]{0:T(128)S(1)} %multiply_reduce_fusion.1), channel_id=1, replica_groups=mesh['grp'=4,'kv_0'=4,'kv_1'=4,'tp'=2] {'kv_0','kv_1'}, use_global_device_ids=true, to_apply=%region_2.0 | all-reduce | flops 128 | bytes 1024 | tf_op jit(solution)/shard_map/psum | solution.py:185
  139.8 61.1 %all-reduce.4.cloned.1.call-done = f32[128,2048]{1,0:T(8,128)} async-done(((f32[128,2048]{1,0:T(8,128)}), f32[128,2048]{1,0:T(8,128)}) %all-reduce.4.cloned.1.call-update) | async-done | bytes 1048592 | tf_op jit(solution)/shard_map/psum | solution.py:185
  205.5 5.0 gather_fusion.4
  216.3 4.7 copy.150
  227.0 4.7 copy.155
  231.7 6.9 %fusion.17 = f32[24,4,4,128]{3,2,1,0:T(4,128)S(1)} fusion(bf16[24,128,4,128]{1,3,2,0:T(8,128)(2,1)} %bitcast.217, f32[24,4,4,128]{3,2,1,0:T(4,128)S(1)} %get-tuple-element.40, f32[24,4,4]{2,1,0:T(4,128)S(1)} %broadcast_select_fusion.3, pred[24,128]{1,0:T(8,128)(4,1)S(1)} %iota_compare_fusion), kind=kOutput, calls=%fused_computation.52 | convolution fusion | flops 75595776 | bytes 3543552 | tf_op jit(solution)/shard_map/ikgt,itkd->ikgd/dot_general | solution.py:144
  241.4 9.3 %all_gather.25 = f32[4,128,16]{1,2,0:T(8,128)S(1)} all-gather(f32[1,128,16]{1,2,0:T(8,128)S(1)} %bitcast.229), channel_id=1, replica_groups=mesh['grp'=4,'kv_0'=4,'kv_1'=4,'tp'=2] {'kv_0'}, dimensions={0}, use_global_device_ids=true | all-gather | bytes 40960 | tf_op jit(solution)/shard_map/all_gather | solution.py:32
  251.3 38.9 %all-gather.4.cloned.1.call-done = f32[4,128,16,128]{3,2,1,0:T(8,128)} async-done(((f32[1,128,16,128]{3,2,1,0:T(8,128)}), f32[4,128,16,128]{3,2,1,0:T(8,128)}) %all-gather.4.cloned.1.call-update) | async-done | bytes 4194320 | tf_op jit(solution)/shard_map/all_gather | solution.py:32
  290.2 4.8 fusion.3
  297.1 9.0 %all-gather = f32[512,16]{0,1:T(8,128)S(1)} all-gather(f32[128,16]{0,1:T(8,128)S(1)} %convolution_add_fusion.1), channel_id=2, replica_groups=mesh['grp'=4,'kv_0'=4,'kv_1'=4,'tp'=2] {'kv_0'}, dimensions={0}, use_global_device_ids=true | all-gather | bytes 40960 | tf_op jit(solution)/shard_map/all_gather | solution.py:32
  306.2 10.8 %all_gather.27 = f32[4,128,16]{1,2,0:T(8,128)S(1)} all-gather(f32[1,128,16]{1,2,0:T(8,128)S(1)} %get-tuple-element.15), channel_id=1, replica_groups=mesh['grp'=4,'kv_0'=4,'kv_1'=4,'tp'=2] {'kv_1'}, dimensions={0}, use_global_device_ids=true | all-gather | bytes 40960 | tf_op jit(solution)/shard_map/all_gather | solution.py:32
  317.0 10.6 %all_gather.30 = f32[4,128,16]{1,2,0:T(8,128)S(1)} all-gather(f32[1,128,16]{1,2,0:T(8,128)S(1)} %get-tuple-element.14), channel_id=1, replica_groups=mesh['grp'=4,'kv_0'=4,'kv_1'=4,'tp'=2] {'kv_1'}, dimensions={0}, use_global_device_ids=true | all-gather | bytes 40960 | tf_op jit(solution)/shard_map/all_gather | solution.py:32
  327.6 16.7 %all-gather.6.cloned.1.call-done = f32[4,128,16,128]{3,2,1,0:T(8,128)} async-done(((f32[1,128,16,128]{3,2,1,0:T(8,128)}), f32[4,128,16,128]{3,2,1,0:T(8,128)}) %all-gather.6.cloned.1.call-update) | async-done | bytes 4194320 | tf_op jit(solution)/shard_map/all_gather | solution.py:32
  358.3 61.2 %all-reduce.6.cloned.1.call-done = bf16[128,4096]{1,0:T(8,128)(2,1)} async-done(((bf16[128,4096]{1,0:T(8,128)(2,1)}), bf16[128,4096]{1,0:T(8,128)(2,1)}) %all-reduce.6.cloned.1.call-update) | async-done | bytes 1048592 | tf_op jit(solution)/shard_map/psum | solution.py:23
  419.5 47.8 %all-reduce.8.cloned.1.call-done = bf16[128,4096]{1,0:T(8,128)(2,1)} async-done(((bf16[128,4096]{1,0:T(8,128)(2,1)}), bf16[128,4096]{1,0:T(8,128)(2,1)}) %all-reduce.8.cloned.1.call-update) | async-done | bytes 1048592 | tf_op jit(solution)/shard_map/psum | solution.py:23
  472.4 6.0 %convolution_convert_fusion = bf16[128,4096]{1,0:T(8,128)(2,1)S(1)} fusion(bf16[448,4096]{1,0:T(8,128)(2,1)} %param.26, bf16[4096,448]{0,1:T(8,128)(2,1)} %param.25, f32[4096]{0:T(1024)S(1)} %copy-done.7, bf16[128,4096]{1,0:T(8,128)(2,1)S(1)} %copy-done.2, f32[128,448]{0,1:T(8,128)S(1)} %convolution_multiply_fusion.1, f32[128]{0:T(128)S(1)} %add_rsqrt_fusion), kind=kOutput, calls=%fused_computation.7 | convolution fusion | flops 942022656 | bytes 9683456 | tf_op jit(solution)/shard_map/dot_general | solution.py:224
  479.6 9.0 %all-to-all-start.2 = ((bf16[32,4,4096]{2,1,0:T(4,128)(2,1)}), bf16[32,4,4096]{2,1,0:T(4,128)(2,1)S(1)}, u32[]{:S(2)}, u32[]{:S(2)}) async-start(bf16[32,4,4096]{2,1,0:T(4,128)(2,1)} %reshape.671), calls=%async_computation.2 | async-start | bytes 2097152 | tf_op jit(solution)/shard_map/all_to_all | solution.py:46
  488.7 4.8 fusion.92
  495.0 10.6 %all-to-all-done.2 = bf16[32,4,4096]{2,1,0:T(4,128)(2,1)S(1)} async-done(((bf16[32,4,4096]{2,1,0:T(4,128)(2,1)}), bf16[32,4,4096]{2,1,0:T(4,128)(2,1)S(1)}, u32[]{:S(2)}, u32[]{:S(2)}) %all-to-all-start.2) | async-done | bytes 1048608 | tf_op jit(solution)/shard_map/all_to_all | solution.py:46
  (132 shorter events, 61.7 us)
Async XLA Ops:
  7.2 95.8 %copy-start = (bf16[256,2048]{1,0:T(8,128)(2,1)S(1)}, bf16[256,2048]{1,0:T(8,128)(2,1)}, u32[]{:S(2)}) copy-start(bf16[256,2048]{1,0:T(8,128)(2,1)} %param.22) | copy-start | bytes 3145732
  20.1 68.0 %all-to-all-start = ((bf16[16,2,128,512]{3,2,1,0:T(8,128)(2,1)}), bf16[16,2,128,512]{3,2,1,0:T(8,128)(2,1)}, u32[]{:S(2)}, u32[]{:S(2)}) async-start(bf16[16,2,128,512]{3,2,1,0:T(8,128)(2,1)} %broadcast_select_fusion.2), calls=%async_computation | async-start | bytes 8388608 | tf_op jit(solution)/shard_map/all_to_all | solution.py:94
  97.8 5.3 %copy-start.6 = (bf16[128,256]{1,0:T(8,128)(2,1)S(1)}, bf16[128,256]{1,0:T(8,128)(2,1)}, u32[]{:S(2)}) copy-start(bf16[128,256]{1,0:T(8,128)(2,1)} %param.19) | copy-start | bytes 196612
  97.8 5.3 %copy-start.8 = (f32[256]{0:T(256)S(1)}, f32[256]{0:T(256)}, u32[]{:S(2)}) copy-start(f32[256]{0:T(256)} %param.20) | copy-start | bytes 3076
  97.8 6.7 %copy-start.9 = (s32[1,16]{1,0:T(1,128)S(1)}, s32[1,16]{1,0:T(1,128)}, u32[]{:S(2)}) copy-start(s32[1,16]{1,0:T(1,128)} %param.33) | copy-start | bytes 196
  97.8 6.7 %copy-start.10 = (s32[1,8]{1,0:T(1,128)S(1)}, s32[1,8]{1,0:T(1,128)}, u32[]{:S(2)}) copy-start(s32[1,8]{1,0:T(1,128)} %param.29) | copy-start | bytes 100
  97.8 7.0 %copy-start.5 = (bf16[128,2,512]{2,1,0:T(2,128)(2,1)S(1)}, bf16[128,2,512]{2,1,0:T(2,128)(2,1)}, u32[]{:S(2)}) copy-start(bf16[128,2,512]{2,1,0:T(2,128)(2,1)} %param.35) | copy-start | bytes 786436
  97.8 107.8 %all-to-all-start.1 = ((bf16[16,2,128,512]{3,2,1,0:T(8,128)(2,1)}), bf16[16,2,128,512]{3,2,1,0:T(8,128)(2,1)}, u32[]{:S(2)}, u32[]{:S(2)}) async-start(bf16[16,2,128,512]{3,2,1,0:T(8,128)(2,1)} %broadcast_select_fusion.1), calls=%async_computation.1 | async-start | bytes 8388608 | tf_op jit(solution)/shard_map/all_to_all | solution.py:110
  103.0 2.2 copy-start.11
  103.0 2.2 copy-start.12
  103.0 98.0 %all-reduce.4.cloned.1.call-start = ((), (), s32[]{:S(2)}) async-start(), calls=%async_computation.3 | async-start | bytes 2097152 | tf_op jit(solution)/shard_map/psum | solution.py:185
  104.4 185.8 %all-gather.4.cloned.1.call-start = ((), (), s32[]{:S(2)}) async-start(), calls=%async_computation.4 | async-start | bytes 5242880 | tf_op jit(solution)/shard_map/all_gather | solution.py:32
  210.6 2.9 copy-start.3
  241.2 103.0 %all-gather.6.cloned.1.call-start = ((), (), s32[]{:S(2)}) async-start(), calls=%async_computation.5 | async-start | bytes 5242880 | tf_op jit(solution)/shard_map/all_gather | solution.py:32
  250.7 44.4 %copy-start.4 = (bf16[16,8,4096]{2,1,0:T(8,128)(2,1)S(1)}, bf16[16,8,4096]{2,1,0:T(8,128)(2,1)}, u32[]{:S(2)}) copy-start(bf16[16,8,4096]{2,1,0:T(8,128)(2,1)} %param.23) | copy-start | bytes 3145732
  295.0 124.5 %all-reduce.6.cloned.1.call-start = ((), (), s32[]{:S(2)}) async-start(), calls=%async_computation.6 | async-start | bytes 2097152 | tf_op jit(solution)/shard_map/psum | solution.py:23
  356.2 112.7 %copy-start.7 = (f32[4096]{0:T(1024)S(1)}, f32[4096]{0:T(1024)}, u32[]{:S(2)}) copy-start(f32[4096]{0:T(1024)} %param.21) | copy-start | bytes 49156
  358.2 109.0 %all-reduce.8.cloned.1.call-start = ((), (), s32[]{:S(2)}) async-start(), calls=%async_computation.7 | async-start | bytes 2097152 | tf_op jit(solution)/shard_map/psum | solution.py:23
  467.3 5.1 copy-start.2
  479.6 25.9 %all-to-all-start.2 = ((bf16[32,4,4096]{2,1,0:T(4,128)(2,1)}), bf16[32,4,4096]{2,1,0:T(4,128)(2,1)S(1)}, u32[]{:S(2)}, u32[]{:S(2)}) async-start(bf16[32,4,4096]{2,1,0:T(4,128)(2,1)} %reshape.671), calls=%async_computation.2 | async-start | bytes 2097152 | tf_op jit(solution)/shard_map/all_to_all | solution.py:46
  488.6 18.9 %copy-start.1 = (bf16[256,2048]{1,0:T(8,128)(2,1)S(1)}, bf16[256,2048]{1,0:T(8,128)(2,1)}, u32[]{:S(2)}) copy-start(bf16[256,2048]{1,0:T(8,128)(2,1)} %param.22) | copy-start | bytes 3145732
Sparse Core Ops, SparseCore 0:
  107.0 93.8 all-reduce.3
  241.4 48.7 all-gather.3
  295.1 49.0 all-gather.5
  358.4 61.0 all-reduce.5
  421.7 45.5 all-reduce.7
